TPU v7x, 32 devices: a whole 2x2x4 slice. The times are simulated.
32 devices in a mesh: gx: 2 (over y), gy: 4 (over z), gz: 4 (over x, core).
Axes of the slice: x: 2, y: 2, z: 4, core: 2. Of those that a mesh axis runs over, the one named last changes fastest.
Arguments:
- forcing: float32 [3, 16, 64, 512], P(None, 'gx', 'gy', 'gz'), may hold values from -8 to 8
- viscosity: float32 [16, 64, 512], P('gx', 'gy', 'gz'), may hold values from 0.001 to 1000
Outputs:
- solution: float32 [3, 16, 64, 512], P(None, 'gx', 'gy', 'gz')
- residual: float32 [3, 16, 64, 512], P(None, 'gx', 'gy', 'gz')
All inputs are finite; a program needn't handle non-finite values.
Results may differ from a plain program's by a relative error of at most 0.00017.
Values sent between devices are 32-bit elements; how exact they have to be, the bound alone decides.
A program may use at most 64 MiB of HBM per device.

v0:
```python
import jax
import jax.numpy as jnp
from jax import lax
from jax.sharding import PartitionSpec as P

ITERS = 3
CSWEEPS = 4


reaction = 1.0
relaxation = 2.0 / 3.0
neighbours = ((1, 0, 0), (-1, 0, 0), (0, 1, 0), (0, -1, 0), (0, 0, 1), (0, 0, -1))


def with_halo(x, sides, width):
    for axis, dim in sides:
        count, length = (lax.axis_size(axis), x.shape[dim])
        up = [(i, (i + 1) % count) for i in range(count - 1)]
        down = [(j, i) for i, j in up]
        last = lax.slice_in_dim(x, length - width, length, axis=dim)
        initial = lax.slice_in_dim(x, 0, width, axis=dim)
        before = lax.ppermute(last, axis, up)
        after = lax.ppermute(initial, axis, down)
        x = jnp.concatenate([before, x, after], axis=dim)
    return x


def window(padded, offset, extent):
    return padded[
        ...,
        1 + offset[0] : 1 + offset[0] + extent[0],
        1 + offset[1] : 1 + offset[1] + extent[1],
        1 + offset[2] : 1 + offset[2] + extent[2],
    ]


def viscous(values, padded_values, viscosity, padded_visc, mass_term, face_term):
    extent = viscosity.shape
    summed = mass_term * values
    for offset in neighbours:
        beside = window(padded_visc, offset, extent)
        across = window(padded_values, offset, extent)
        summed = summed + face_term * (viscosity + beside) * (values - across)
    return summed


def diagonal_of(viscosity, padded_visc, mass_term, face_term):
    summed = jnp.full(viscosity.shape, mass_term, jnp.float32)
    for offset in neighbours:
        summed = summed + face_term * (viscosity + window(padded_visc, offset, viscosity.shape))
    return summed


def restrict(values):
    extent = values.shape
    return values.reshape(extent[0], extent[1] // 2, 2, extent[2] // 2, 2, extent[3] // 2, 2).sum(
        axis=(2, 4, 6)
    )


def prolong(values):
    return jnp.repeat(jnp.repeat(jnp.repeat(values, 2, axis=1), 2, axis=2), 2, axis=3)


def coarsen(viscosity):
    extent = viscosity.shape
    return viscosity.reshape(extent[0] // 2, 2, extent[1] // 2, 2, extent[2] // 2, 2).mean(
        axis=(1, 3, 5)
    )


def sweeps(coarse_rhs, diagonal, applier):
    correction = relaxation * coarse_rhs / diagonal
    for counter in range(CSWEEPS - 1):
        correction = correction + relaxation * (coarse_rhs - applier(correction)) / diagonal
    return correction


def precond_product(residual, precond):
    return lax.psum(jnp.sum(residual * precond), ("gx", "gy", "gz"))


def shards(forcing, viscosity):
    padded_visc = with_halo(viscosity, (("gx", 0), ("gy", 1), ("gz", 2)), 1)
    fine_diag = diagonal_of(viscosity, padded_visc, reaction, 0.5)
    coarse_visc = coarsen(viscosity)

    def fine_apply(values):
        padded = with_halo(values, (("gx", 1), ("gy", 2), ("gz", 3)), 1)
        return viscous(values, padded, viscosity, padded_visc, reaction, 0.5)

    group_visc = lax.all_gather(coarse_visc, "gz", axis=2, tiled=True)
    group_pad = with_halo(group_visc, (("gx", 0), ("gy", 1)), 1)
    group_pad = jnp.pad(group_pad, ((0, 0), (0, 0), (1, 1)))
    group_diag = diagonal_of(group_visc, group_pad, 8.0 * reaction, 2.0)
    depth_local = coarse_visc.shape[2]
    offset_z = lax.axis_index("gz") * depth_local

    def group_apply(values):
        padded = with_halo(values, (("gx", 1), ("gy", 2)), 1)
        padded = jnp.pad(padded, ((0, 0), (0, 0), (0, 0), (1, 1)))
        return viscous(values, padded, group_visc, group_pad, 8.0 * reaction, 2.0)

    def coarse_solve(coarse_rhs):
        whole_line = lax.all_gather(coarse_rhs, "gz", axis=3, tiled=True)
        correction = sweeps(whole_line, group_diag, group_apply)
        return lax.dynamic_slice_in_dim(correction, offset_z, depth_local, 3)

    def precondition(residual):
        smoothed = relaxation * residual / fine_diag
        defect = residual - fine_apply(smoothed)
        correction = coarse_solve(restrict(defect))
        smoothed = smoothed + prolong(correction)
        return smoothed + relaxation * (residual - fine_apply(smoothed)) / fine_diag

    solution = jnp.zeros_like(forcing)
    residual = forcing
    precond = precondition(residual)
    product = precond_product(residual, precond)
    direction = precond
    for iteration in range(ITERS):
        applied = fine_apply(direction)
        alpha_step = product / lax.psum(jnp.sum(direction * applied), ("gx", "gy", "gz"))
        solution = solution + alpha_step * direction
        residual = residual - alpha_step * applied
        if iteration + 1 < ITERS:
            precond = precondition(residual)
            product_next = precond_product(residual, precond)
            direction = precond + product_next / product * direction
            product = product_next
    return (solution, residual)


def solution(mesh):
    return jax.shard_map(
        shards,
        mesh=mesh,
        in_specs=(P(None, "gx", "gy", "gz"), P("gx", "gy", "gz")),
        out_specs=(P(None, "gx", "gy", "gz"), P(None, "gx", "gy", "gz")),
        check_vma=False,
    )
```

profile of v0, /device:TPU:0, one launch (start us, length us, event | category | flops | bytes accessed | tf_op | source)
XLA Modules:
  0.0 754.0 jit_solution(5678509347087031177)
XLA Ops:
  1.3 4.9 collective-permute-start.1
  7.5 6.3 reshape.58
  21.4 7.2 all_gather.13
  32.5 4.5 collective-permute-start.13
  38.6 4.5 collective-permute-start.7
  44.5 4.5 collective-permute-start.15
  50.4 4.5 collective-permute-start.9
  66.7 13.9 %reshape.57 = f32[3,4,2,8,2,64,2]{6,5,4,3,2,1,0:T(8,128)} reshape(f32[3,8,16,128]{3,2,1,0:T(8,128)S(1)} %fusion.162) | data formatting | bytes 393216 | tf_op jit(solution)/shard_map/reshape | solution.py:56
  80.7 5.5 reduce_sum.90
  86.4 19.3 %all_gather.12 = f32[3,4,8,256]{2,1,0,3:T(4,128)S(1)} all-gather(f32[3,4,8,64]{2,1,0,3:T(4,128)S(1)} %copy.996), channel_id=1, replica_groups=mesh['gx'=2,'gy'=4,'gz'=4] {'gz'}, dimensions={3}, use_global_device_ids=true | all-gather | bytes 122880 | tf_op jit(solution)/shard_map/all_gather | solution.py:105
  106.3 4.5 collective-permute-start.17
  112.4 4.2 collective-permute-done.16
  121.6 4.2 collective-permute-done.18
  129.4 4.2 collective-permute-done.20
  138.6 4.2 collective-permute-done.22
  146.4 4.2 collective-permute-done.24
  154.0 4.2 collective-permute-done.26
  165.0 4.2 collective-permute-done.28
  186.2 4.2 collective-permute-done.34
  204.8 46.7 %all-reduce.10 = (f32[]{:T(128)}, f32[]{:T(128)}) all-reduce(f32[]{:T(128)} %get-tuple-element.13, f32[]{:T(128)} %get-tuple-element.12), channel_id=1, replica_groups=mesh['gx'=2,'gy'=4,'gz'=4] {'gx','gy','gz'}, use_global_device_ids=true, to_apply=%region_3.4 | all-reduce | flops 2 | bytes 16 | tf_op jit(solution)/shard_map/psum | solution.py:80
  252.9 4.4 collective-permute-start.41
  258.7 4.2 collective-permute-done.40
  278.6 13.9 %reshape.62 = f32[3,4,2,8,2,64,2]{6,5,4,3,2,1,0:T(8,128)} reshape(f32[3,8,16,128]{3,2,1,0:T(8,128)S(1)} %fusion.103) | data formatting | bytes 393216 | tf_op jit(solution)/shard_map/reshape | solution.py:56
  292.6 5.5 reduce_sum.94
  298.3 18.5 %all_gather.14 = f32[3,4,8,256]{2,1,0,3:T(4,128)S(1)} all-gather(f32[3,4,8,64]{2,1,0,3:T(4,128)S(1)} %copy.1016), channel_id=1, replica_groups=mesh['gx'=2,'gy'=4,'gz'=4] {'gz'}, dimensions={3}, use_global_device_ids=true | all-gather | bytes 122880 | tf_op jit(solution)/shard_map/all_gather | solution.py:105
  320.5 4.2 collective-permute-done.46
  328.8 4.2 collective-permute-done.48
  336.6 4.2 collective-permute-done.50
  344.2 4.2 collective-permute-done.52
  352.0 4.2 collective-permute-done.54
  370.7 4.2 collective-permute-done.58
  389.3 41.5 %psum.44 = f32[]{:T(128)} all-reduce(f32[]{:T(128)} %get-tuple-element.24), channel_id=1, replica_groups=mesh['gx'=2,'gy'=4,'gz'=4] {'gx','gy','gz'}, use_global_device_ids=true, to_apply=%region_8.9 | all-reduce | flops 1 | bytes 8 | tf_op jit(solution)/shard_map/psum | solution.py:80
  432.1 4.4 collective-permute-start.65
  438.1 4.2 collective-permute-done.64
  458.5 43.7 %psum.45 = f32[]{:T(128)} all-reduce(f32[]{:T(128)} %get-tuple-element.22), channel_id=1, replica_groups=mesh['gx'=2,'gy'=4,'gz'=4] {'gx','gy','gz'}, use_global_device_ids=true, to_apply=%region_10.11 | all-reduce | flops 1 | bytes 8 | tf_op jit(solution)/shard_map/psum | solution.py:123
  503.6 4.4 collective-permute-start.71
  509.5 4.2 collective-permute-done.70
  528.8 13.9 %reshape.66 = f32[3,4,2,8,2,64,2]{6,5,4,3,2,1,0:T(8,128)} reshape(f32[3,8,16,128]{3,2,1,0:T(8,128)S(1)} %fusion.44) | data formatting | bytes 393216 | tf_op jit(solution)/shard_map/reshape | solution.py:56
  542.8 5.5 reduce_sum.97
  548.5 18.5 %all_gather.15 = f32[3,4,8,256]{2,1,0,3:T(4,128)S(1)} all-gather(f32[3,4,8,64]{2,1,0,3:T(4,128)S(1)} %copy.1024), channel_id=1, replica_groups=mesh['gx'=2,'gy'=4,'gz'=4] {'gz'}, dimensions={3}, use_global_device_ids=true | all-gather | bytes 122880 | tf_op jit(solution)/shard_map/all_gather | solution.py:105
  570.7 4.2 collective-permute-done.76
  586.8 4.2 collective-permute-done.80
  602.9 4.2 collective-permute-done.84
  619.7 4.2 collective-permute-done.88
  638.3 41.5 %psum.46 = f32[]{:T(128)} all-reduce(f32[]{:T(128)} %get-tuple-element.18), channel_id=1, replica_groups=mesh['gx'=2,'gy'=4,'gz'=4] {'gx','gy','gz'}, use_global_device_ids=true, to_apply=%region_13.14 | all-reduce | flops 1 | bytes 8 | tf_op jit(solution)/shard_map/psum | solution.py:80
  681.1 4.4 collective-permute-start.95
  687.0 4.2 collective-permute-done.94
  707.5 43.7 %psum.47 = f32[]{:T(128)} all-reduce(f32[]{:T(128)} %get-tuple-element.16), channel_id=1, replica_groups=mesh['gx'=2,'gy'=4,'gz'=4] {'gx','gy','gz'}, use_global_device_ids=true, to_apply=%region_15.16 | all-reduce | flops 1 | bytes 8 | tf_op jit(solution)/shard_map/psum | solution.py:123
  (317 shorter events, 261.9 us)
Async XLA Ops:
  1.3 15.2 %collective-permute-start.1 = (f32[1,16,128]{2,1,0:T(8,128)S(1)}, f32[1,16,128]{2,1,0:T(8,128)S(1)}, u32[]{:S(2)}, u32[]{:S(2)}) collective-permute-start(f32[1,16,128]{2,1,0:T(8,128)S(1)} %get-tuple-element.143), channel_id=1, source_target_pairs={{0,16},{1,17},{2,18},{3,19},{4,20},{5,21},{6,22},{7,23},{8,24},{9,... | collective-permute-start | bytes 24584 | tf_op jit(solution)/shard_map/ppermute | solution.py:22
  6.2 10.4 %collective-permute-start = (f32[1,16,128]{2,1,0:T(8,128)S(1)}, f32[1,16,128]{2,1,0:T(8,128)S(1)}, u32[]{:S(2)}, u32[]{:S(2)}) collective-permute-start(f32[1,16,128]{2,1,0:T(8,128)S(1)} %get-tuple-element.144), channel_id=1, source_target_pairs={{16,0},{17,1},{18,2},{19,3},{20,4},{21,5},{22,6},{23,7},{24,8},{25... | collective-permute-start | bytes 24584 | tf_op jit(solution)/shard_map/ppermute | solution.py:23
  16.6 12.1 %collective-permute-start.3 = (f32[10,1,128]{2,1,0:T(1,128)S(1)}, f32[10,1,128]{2,1,0:T(1,128)S(1)}, u32[]{:S(2)}, u32[]{:S(2)}) collective-permute-start(f32[10,1,128]{2,1,0:T(1,128)S(1)} %get-tuple-element.141), channel_id=1, source_target_pairs={{0,4},{4,8},{8,12},{1,5},{5,9},{9,13},{2,6},{6,10},{10,14},{3,7},{... | collective-permute-start | bytes 15368 | tf_op jit(solution)/shard_map/ppermute | solution.py:22
  20.1 8.7 %collective-permute-start.2 = (f32[10,1,128]{2,1,0:T(1,128)S(1)}, f32[10,1,128]{2,1,0:T(1,128)S(1)}, u32[]{:S(2)}, u32[]{:S(2)}) collective-permute-start(f32[10,1,128]{2,1,0:T(1,128)S(1)} %get-tuple-element.142), channel_id=1, source_target_pairs={{4,0},{8,4},{12,8},{5,1},{9,5},{13,9},{6,2},{10,6},{14,10},{7,3},{... | collective-permute-start | bytes 15368 | tf_op jit(solution)/shard_map/ppermute | solution.py:23
  28.9 9.4 %collective-permute-start.5 = (f32[10,18,1]{2,1,0:T(8,128)S(1)}, f32[10,18,1]{2,1,0:T(8,128)S(1)}, u32[]{:S(2)}, u32[]{:S(2)}) collective-permute-start(f32[10,18,1]{2,1,0:T(8,128)S(1)} %get-tuple-element.121), channel_id=1, source_target_pairs={{0,1},{1,2},{2,3},{4,5},{5,6},{6,7},{8,9},{9,10},{10,11},{12,13},{... | collective-permute-start | bytes 2168 | tf_op jit(solution)/shard_map/ppermute | solution.py:22
  31.2 7.2 collective-permute-start.4
  32.5 11.9 %collective-permute-start.13 = (f32[1,8,256]{2,1,0:T(8,128)S(1)}, f32[1,8,256]{2,1,0:T(8,128)S(1)}, u32[]{:S(2)}, u32[]{:S(2)}) collective-permute-start(f32[1,8,256]{2,1,0:T(8,128)S(1)} %get-tuple-element.147), channel_id=1, source_target_pairs={{0,16},{1,17},{2,18},{3,19},{4,20},{5,21},{6,22},{7,23},{8,24},{9,... | collective-permute-start | bytes 24584 | tf_op jit(solution)/shard_map/ppermute | solution.py:22
  37.0 7.4 collective-permute-start.12
  38.6 11.7 %collective-permute-start.7 = (f32[3,1,16,128]{3,2,1,0:T(8,128)S(1)}, f32[3,1,16,128]{3,2,1,0:T(8,128)S(1)}, u32[]{:S(2)}, u32[]{:S(2)}) collective-permute-start(f32[3,1,16,128]{3,2,1,0:T(8,128)S(1)} %get-tuple-element.101), channel_id=1, source_target_pairs={{0,16},{1,17},{2,18},{3,19},{4,20},{5,21},{6,22},{7,23},{8,24},{9,... | collective-permute-start | bytes 73736 | tf_op jit(solution)/shard_map/ppermute | solution.py:22
  43.1 7.2 collective-permute-start.6
  44.5 11.8 %collective-permute-start.15 = (f32[6,1,256]{2,1,0:T(1,128)S(1)}, f32[6,1,256]{2,1,0:T(1,128)S(1)}, u32[]{:S(2)}, u32[]{:S(2)}) collective-permute-start(f32[6,1,256]{2,1,0:T(1,128)S(1)} %get-tuple-element.145), channel_id=1, source_target_pairs={{0,4},{4,8},{8,12},{1,5},{5,9},{9,13},{2,6},{6,10},{10,14},{3,7},{... | collective-permute-start | bytes 18440 | tf_op jit(solution)/shard_map/ppermute | solution.py:22
  49.0 7.2 collective-permute-start.14
  50.4 6.0 collective-permute-start.9
  54.9 5.6 collective-permute-start.8
  106.3 6.1 collective-permute-start.17
  110.9 5.7 collective-permute-start.16
  120.2 5.7 collective-permute-start.18
  127.9 5.7 collective-permute-start.20
  137.1 5.7 collective-permute-start.22
  144.9 5.7 collective-permute-start.24
  152.6 5.7 collective-permute-start.26
  163.5 5.7 collective-permute-start.28
  171.2 5.6 collective-permute-start.30
  184.7 5.7 collective-permute-start.34
  192.4 5.6 collective-permute-start.36
  252.9 5.9 collective-permute-start.41
  257.2 5.7 collective-permute-start.40
  266.8 5.6 collective-permute-start.42
  319.0 5.7 collective-permute-start.46
  327.4 5.7 collective-permute-start.48
  335.1 5.7 collective-permute-start.50
  342.8 5.7 collective-permute-start.52
  350.5 5.7 collective-permute-start.54
  358.2 5.7 collective-permute-start.56
  369.2 5.7 collective-permute-start.58
  432.1 5.9 collective-permute-start.65
  436.6 5.7 collective-permute-start.64
  503.6 5.9 collective-permute-start.71
  508.0 5.7 collective-permute-start.70
  569.2 5.7 collective-permute-start.76
  577.5 5.7 collective-permute-start.78
  585.3 5.7 collective-permute-start.80
  593.6 5.7 collective-permute-start.82
  601.4 5.7 collective-permute-start.84
  609.0 5.7 collective-permute-start.86
  618.2 5.7 collective-permute-start.88
  681.1 5.9 collective-permute-start.95
  685.5 5.7 collective-permute-start.94
  (56 other events, 284.8 us)
where the time goes:
time: 757 us; the launch traced here: 754 us
  blocking collectives  281 us (37%)
  starting transfers between devices  208 us (27%)
  waiting for transfers between devices  164 us (22%)
  local copies, waits for them, and re-layouts  60.2 us (8%)
  other arithmetic  32.7 us (4%)
  between operations  8.96 us (1%)
    ppermute x50, waiting for transfers between devices, with_halo(): after = lax.ppermute(initial, axis, down)  147 us
    ppermute x50, starting transfers between devices, with_halo(): before = lax.ppermute(last, axis, up)  143 us
    psum x3, blocking collectives, precond_product(): return lax.psum(jnp.sum(residual * precond), ('gx', 'gy', 'gz'))  130 us
    psum x2, blocking collectives, shards(): lax.psum(jnp.sum(direction * applied), ('gx', 'gy', 'gz'))  87.4 us
    ppermute x50, starting transfers between devices, with_halo(): after = lax.ppermute(initial, axis, down)  64.8 us
    all_gather x3, blocking collectives, coarse_solve(): whole_line = lax.all_gather(coarse_rhs, 'gz', axis=3, tiled=True)  56.3 us
    reshape x3, local copies, waits for them, and re-layouts, restrict(): values.reshape(extent[0], extent[1] // 2, 2, extent[2] // 2, 2, extent[3]...  41.8 us
    ppermute x50, waiting for transfers between devices, with_halo(): before = lax.ppermute(last, axis, up)  16.6 us
  transfers between devices with their start and end apart: 100, of which 77 were waited for; matrix products, arithmetic and copies ran while one was open for 1% of the time, Pallas kernels for 0%

commit v1 on v0

v1 whole, which is shorter than its diff:
```python
import functools
import jax
import jax.numpy as jnp
from jax import lax
from jax.experimental import pallas as pl
from jax.experimental.pallas import tpu as pltpu
from jax.sharding import PartitionSpec as P

ITERS = 3
CSWEEPS = 4
AXES = ("gx", "gy", "gz")
MESH = pl.DeviceIdType.MESH
relax = 2.0 / 3.0
ROUNDS = 2 + ITERS * (CSWEEPS + 2)


def kernel(sizes, f_ref, v_ref, x_out, r_out, sx, sy, sz, rx, ry, rz, cf, fw, cc, cw, r, u, w, p, s, q, z,
           ssend, srecv, red_src, red_dst, rsend, rrecv):
    NC, X, Y, Z = f_ref.shape
    T = Y // 8
    place = [lax.axis_index(a) for a in AXES]
    total = [sizes[a] for a in AXES]
    gx_n, gy_n, gz_n = total
    plane = [(i, j) for i in range(gx_n) for j in range(gz_n) if (i, j) != (0, 0)]

    def plane_peer(i, j):
        return {"gx": lax.rem(place[0] + i, gx_n), "gz": lax.rem(place[2] + j, gz_n)}

    def line_peer(i):
        return {"gy": lax.rem(place[1] + i, gy_n)}

    barrier = pltpu.get_barrier_semaphore()
    count = len(plane) + gy_n - 1
    for i, j in plane:
        pl.semaphore_signal(barrier, inc=1, device_id=plane_peer(i, j), device_id_type=MESH)
    for i in range(1, gy_n):
        pl.semaphore_signal(barrier, inc=1, device_id=line_peer(i), device_id_type=MESH)

    for a, buf in enumerate((rx, ry, rz)):
        @pl.when(place[a] == 0)
        def _():
            buf[:, 0] = jnp.zeros_like(buf[:, 0])

        @pl.when(place[a] == total[a] - 1)
        def _():
            buf[:, 1] = jnp.zeros_like(buf[:, 1])

    lane2 = lax.broadcasted_iota(jnp.int32, (8, Z), 1)
    iy = lax.broadcasted_iota(jnp.int32, (1, Y, Z), 1)
    iz = lax.broadcasted_iota(jnp.int32, (1, Y, Z), 2)

    def copies(slot, nc):
        made = []
        for a, (src, dst) in enumerate(((sx, rx), (sy, ry), (sz, rz))):
            for up in (0, 1):
                ok = place[a] < total[a] - 1 if up else place[a] > 0
                if a == 2:
                    source, target = src.at[slot], dst.at[slot, 1 - up]
                else:
                    source = src.at[slot, up, pl.ds(0, nc)]
                    target = dst.at[slot, 1 - up, pl.ds(0, nc)]
                copy = pltpu.make_async_remote_copy(
                    src_ref=source, dst_ref=target, send_sem=ssend.at[slot, 2 * a + up],
                    recv_sem=srecv.at[slot, 2 * a + 1 - up],
                    device_id={AXES[a]: place[a] + (1 if up else -1)}, device_id_type=MESH)
                if a == 2:
                    mine = dst.at[slot, up]
                else:
                    mine = dst.at[slot, up, pl.ds(0, nc)]
                arrive = pltpu.make_async_remote_copy(
                    src_ref=source, dst_ref=mine, send_sem=ssend.at[slot, 2 * a + up],
                    recv_sem=srecv.at[slot, 2 * a + up],
                    device_id={AXES[a]: place[a] + (1 if up else -1)}, device_id_type=MESH)
                made.append((ok, copy, arrive))
        return made

    used = []

    def launch(slot, comps, unit):
        used.append((slot, len(comps)))
        nx = comps[0].shape[0]
        made = copies(slot, len(comps))
        for c, v in enumerate(comps):
            sx[slot, 0, c] = v[0]
            sx[slot, 1, c] = v[nx - 1]
        for ok, copy, _ in made[0:2]:
            pl.when(ok)(copy.start)
        for c, v in enumerate(comps):
            for i in range(X):
                k = i * nx // X
                sy[slot, 0, c, i : i + 1] = v[k, 0:1]
                sy[slot, 1, c, i : i + 1] = v[k, Y - 1 : Y]
        for ok, copy, _ in made[2:4]:
            pl.when(ok)(copy.start)
        which = (lane2 - unit + 2 * unit) // (2 * unit) - 1
        packed = jnp.zeros((8, Z), jnp.float32)
        for c, v in enumerate(comps):
            for i in range(nx):
                for t in range(T):
                    k = (c * nx + i) * T + t
                    rolled = pltpu.roll(v[i, 8 * t : 8 * t + 8], (2 * unit * (k + 1)) % Z, 1)
                    packed = jnp.where((lane2 >= 2 * unit * k + unit), rolled, packed)
        sz[slot] = packed
        for ok, copy, _ in made[4:6]:
            pl.when(ok)(copy.start)

    def land(slot, nc, nx, unit):
        for ok, _, arrive in copies(slot, nc):
            pl.when(ok)(arrive.wait_recv)
        below, above = rz[slot, 0], rz[slot, 1]
        both = jnp.where(lax.rem(lane2, 2 * unit) >= unit, below, pltpu.roll(above, Z - 2 * unit, 1))
        halos = []
        for c in range(nc):
            hz = []
            for i in range(nx):
                parts = []
                for t in range(T):
                    k = (c * nx + i) * T + t
                    parts.append(pltpu.roll(both, (2 * Z - unit - 2 * unit * k) % Z, 1))
                hz.append(jnp.concatenate(parts, axis=0)[None])
            hz = jnp.concatenate(hz, axis=0)
            halos.append((rx[slot, 0, c], rx[slot, 1, c], ry[slot, 0, c], ry[slot, 1, c], hz))
        return halos

    def rows(h, nx):
        h = h[:, None, :]
        if nx != X:
            h = jnp.concatenate([h[i * X // nx][None] for i in range(nx)], axis=0)
        return h

    def beside(v, halo, unit):
        nx = v.shape[0]
        hxm, hxp, hym, hyp, hz = halo
        return (
            jnp.concatenate([v[1:], hxp[None]], axis=0),
            jnp.concatenate([hxm[None], v[:-1]], axis=0),
            jnp.where(iy >= Y - unit, rows(hyp, nx), pltpu.roll(v, Y - unit, 1)),
            jnp.where(iy < unit, rows(hym, nx), pltpu.roll(v, unit, 1)),
            jnp.where(iz >= Z - unit, hz, pltpu.roll(v, Z - unit, 2)),
            jnp.where(iz < unit, hz, pltpu.roll(v, unit, 2)),
        )

    def viscous(v, halo, coef, mass, unit):
        out = v * mass if mass != 1.0 else v
        for d, across in enumerate(beside(v, halo, unit)):
            out = out + coef[d] * (v - across)
        return out

    def pairsum(v):
        v = v.reshape(X // 2, 2, Y, Z)
        v = v[:, 0] + v[:, 1]
        v = v + jnp.where(iy % 2 == 0, pltpu.roll(v, Y - 1, 1), pltpu.roll(v, 1, 1))
        return v + jnp.where(iz % 2 == 0, pltpu.roll(v, Z - 1, 2), pltpu.roll(v, 1, 2))

    def twice(v):
        h = v.shape[0]
        return jnp.broadcast_to(v[:, None], (h, 2) + v.shape[1:]).reshape((2 * h,) + v.shape[1:])

    C = range(NC)
    nxc = X // 2
    visc = v_ref[...]
    cvisc = pairsum(visc) * 0.125
    pl.semaphore_wait(barrier, count)
    launch(0, [visc], 1)
    launch(1, [cvisc], 2)

    (halo,) = land(0, 1, X, 1)
    diag = jnp.ones_like(visc)
    for d, other in enumerate(beside(visc, halo, 1)):
        face = 0.5 * (visc + other)
        cf[d] = face
        diag = diag + face
    fw[...] = relax / diag
    next_slot = [2]

    def take():
        next_slot[0] += 1
        return next_slot[0] - 1

    first = [True]

    def pair(vec, store_m, store_n, middle):
        a = take()
        sm = [vec[c] * fw[...] for c in C]
        launch(a, sm, 1)
        if first[0]:
            first[0] = False
            (ch,) = land(1, 1, nxc, 2)
            cdiag = jnp.full_like(cvisc, 8.0)
            for d, other in enumerate(beside(cvisc, ch, 2)):
                face = 2.0 * (cvisc + other)
                cc[d] = face
                cdiag = cdiag + face
            cw[...] = relax / cdiag
        fine_halo = land(a, NC, X, 1)
        rhs = [pairsum(vec[c] - viscous(sm[c], fine_halo[c], cf, 1.0, 1)) for c in C]
        corr = [rhs[c] * cw[...] for c in C]
        for sweep in range(CSWEEPS - 1):
            b = take()
            launch(b, corr, 2)
            if sweep == 1:
                middle()
            ch = land(b, NC, nxc, 2)
            corr = [corr[c] + cw[...] * (rhs[c] - viscous(corr[c], ch[c], cc, 8.0, 2)) for c in C]
        b = take()
        launch(b, corr, 2)
        ch = land(b, NC, nxc, 2)
        m = []
        for c in C:
            sm2 = sm[c] + twice(corr[c])
            halo = tuple(fine_halo[c][i] + ch[c][i] for i in range(4)) + (fine_halo[c][4] + twice(ch[c][4]),)
            m.append(sm2 + fw[...] * (vec[c] - viscous(sm2, halo, cf, 1.0, 1)))
        b = take()
        launch(b, m, 1)
        for c in C:
            store_m(c, m[c])
        mh = land(b, NC, X, 1)
        for c in C:
            store_n(c, viscous(m[c], mh[c], cf, 1.0, 1))

    def red_copy(n, stage, k):
        if stage == 0:
            i, j = plane[k]
            peer, base = plane_peer(i, j), k
        else:
            peer, base = line_peer(k + 1), len(plane) + k
        return pltpu.make_async_remote_copy(
            src_ref=red_src.at[n, stage], dst_ref=red_dst.at[n, base],
            send_sem=rsend.at[n, base], recv_sem=rrecv.at[n, base],
            device_id=peer, device_id_type=MESH)

    def peers(stage):
        return range(len(plane)) if stage == 0 else range(gy_n - 1)

    def fold(v):
        v = v.reshape(X * T, 8, Z).sum(axis=0)
        return v + pltpu.roll(v, 4, 0)

    sub = lax.broadcasted_iota(jnp.int32, (8, Z), 0)

    def reduce_start(n):
        g = d = 0.0
        for c in C:
            g = g + r[c] * u[c]
            d = d + u[c] * w[c]
        red_src[n, 0] = jnp.where(sub < 4, fold(g), fold(d))
        for k in peers(0):
            red_copy(n, 0, k).start()

    def reduce_middle(n):
        acc = red_src[n, 0]
        for k in peers(0):
            red_copy(n, 0, k).wait_recv()
            acc = acc + red_dst[n, k]
        red_src[n, 1] = acc
        for k in peers(1):
            red_copy(n, 1, k).start()

    def reduce_end(n):
        acc = red_src[n, 1]
        for k in peers(1):
            red_copy(n, 1, k).wait_recv()
            acc = acc + red_dst[n, len(plane) + k]
        g = jnp.sum(jnp.where(sub < 4, acc, 0.0))
        d = jnp.sum(jnp.where(sub < 4, 0.0, acc))
        return jnp.full((1, 1, Z), g), jnp.full((1, 1, Z), d)

    def put(ref):
        def store(c, value):
            ref[c] = value
        return store

    r[...] = f_ref[...]
    pair([f_ref[c] for c in C], put(u), put(w), lambda: None)
    gamma_old = alpha_old = None
    for n in range(ITERS):
        last = n == ITERS - 1
        reduce_start(n)
        fresh = {}
        if not last:
            store_m = lambda c, value: fresh.__setitem__(("m", c), value)
            store_n = lambda c, value: fresh.__setitem__(("n", c), value)
            pair([w[c] for c in C], store_m, store_n, lambda: reduce_middle(n))
        else:
            reduce_middle(n)
        gamma, delta = reduce_end(n)
        if n == 0:
            beta = None
            alpha = gamma / delta
        else:
            beta = gamma / gamma_old
            alpha = gamma / (delta - beta * gamma / alpha_old)
        mix = lambda new, ref, c: new if beta is None else new + beta * ref[c]
        for c in C:
            dn = mix(u[c], p, c)
            an = mix(w[c], s, c)
            x_out[c] = alpha * dn if n == 0 else x_out[c] + alpha * dn
            res = r[c] - alpha * an
            if last:
                r_out[c] = res
                continue
            r[c] = res
            p[c] = dn
            s[c] = an
            qn = mix(fresh["m", c], q, c)
            zn = mix(fresh["n", c], z, c)
            q[c] = qn
            z[c] = zn
            u[c] = u[c] - alpha * qn
            w[c] = w[c] - alpha * zn
        gamma_old, alpha_old = gamma, alpha

    for slot, nc in used:
        for ok, copy, _ in copies(slot, nc):
            pl.when(ok)(copy.wait_send)
    for n in range(ITERS):
        for stage in (0, 1):
            for k in peers(stage):
                red_copy(n, stage, k).wait_send()


def solution(mesh):
    sizes = dict(mesh.shape)

    def shards(forcing, viscosity):
        NC, X, Y, Z = forcing.shape
        f32 = jnp.float32
        whole = pltpu.VMEM((NC, X, Y, Z), f32)
        peers = sizes["gx"] * sizes["gz"] - 1 + sizes["gy"] - 1
        spec = pl.BlockSpec(memory_space=pltpu.VMEM)
        out = jax.ShapeDtypeStruct(forcing.shape, f32)
        dma = pltpu.SemaphoreType.DMA
        halo = [
            pltpu.VMEM((ROUNDS, 2, NC, Y, Z), f32),
            pltpu.VMEM((ROUNDS, 2, NC, X, Z), f32),
        ]
        return pl.pallas_call(
            functools.partial(kernel, sizes),
            out_shape=(out, out),
            in_specs=[spec, spec],
            out_specs=(spec, spec),
            scratch_shapes=halo + [pltpu.VMEM((ROUNDS, 8, Z), f32)] + halo + [
                pltpu.VMEM((ROUNDS, 2, 8, Z), f32),
                pltpu.VMEM((6, X, Y, Z), f32),
                pltpu.VMEM((X, Y, Z), f32),
                pltpu.VMEM((6, X // 2, Y, Z), f32),
                pltpu.VMEM((X // 2, Y, Z), f32),
            ] + [whole] * 7 + [
                dma((ROUNDS, 6)),
                dma((ROUNDS, 6)),
                pltpu.VMEM((ITERS, 2, 8, Z), f32),
                pltpu.VMEM((ITERS, peers, 8, Z), f32),
                dma((ITERS, peers)),
                dma((ITERS, peers)),
            ],
            compiler_params=pltpu.CompilerParams(
                collective_id=0, has_side_effects=True, vmem_limit_bytes=48 * 1024 * 1024
            ),
        )(forcing, viscosity)

    return jax.shard_map(
        shards,
        mesh=mesh,
        in_specs=(P(None, "gx", "gy", "gz"), P("gx", "gy", "gz")),
        out_specs=(P(None, "gx", "gy", "gz"), P(None, "gx", "gy", "gz")),
        check_vma=False,
    )
```

time: 757 us -> 78.6 us (0.10)
  blocking collectives: 281 us -> 0 us
  starting transfers between devices: 208 us -> 0 us
  waiting for transfers between devices: 164 us -> 0 us
  Pallas kernels: 0 us -> 74.6 us
  local copies, waits for them, and re-layouts: 60.2 us -> 3.11 us
  other arithmetic: 32.7 us -> 0 us
  between operations: 8.96 us -> 0.65 us
    psum x5 -> x0, blocking collectives: 217 us -> none  [the longest x3 130 us: precond_product(): return lax.psum(jnp.sum(residual * precond), ('gx', 'gy', 'gz'))]
    ppermute x100 -> x0, starting transfers between devices: 208 us -> none  [the longest x50 143 us: with_halo(): before = lax.ppermute(last, axis, up)]
    ppermute x100 -> x0, waiting for transfers between devices: 164 us -> none  [the longest x50 147 us: with_halo(): after = lax.ppermute(initial, axis, down)]
    pallas_call x0 -> x1, Pallas kernels: none -> 74.6 us  [shards(): pl.pallas_call(functools.partial(kernel, sizes), out_shape=(out, out), in...]
    all_gather x4 -> x0, blocking collectives: 63.5 us -> none  [the longest x3 56.3 us: coarse_solve(): whole_line = lax.all_gather(coarse_rhs, 'gz', axis=3, tiled=True)]
    reshape x10 -> x0, local copies, waits for them, and re-layouts: 52.2 us -> none  [the longest x3 41.8 us: restrict(): values.reshape(extent[0], extent[1] // 2, 2, extent[2] // 2, 2, extent[3]...]
    reduce_sum x9 -> x0, other arithmetic: 23.7 us -> none  [the longest x3 16.5 us: restrict(): values.reshape(extent[0], extent[1] // 2, 2, extent[2] // 2, 2, extent[3]...]
  transfers between devices with their start and end apart: 100 -> 0, of which waited for: 77 -> 0; matrix products, arithmetic and copies ran while one was open for 1% -> 0% of each run, Pallas kernels for 0% -> 0%
where the time goes in v1:
time: 78.6 us; the launch traced here: 78.4 us
  Pallas kernels  74.6 us (95%)
  local copies, waits for them, and re-layouts  3.11 us (4%)
    pallas_call x1, Pallas kernels, shards(): pl.pallas_call(functools.partial(kernel, sizes), out_shape=(out, out), in...  74.6 us
    unnamed x6, local copies, waits for them, and re-layouts  3.11 us

profile of v1, /device:TPU:0, one launch (start us, length us, event | category | flops | bytes accessed | tf_op | source)
XLA Modules:
  0.0 78.4 jit_solution(11594918403433619934)
XLA Ops:
  0.6 0.0 copy-start
  0.6 0.9 %copy-done = f32[3,8,16,128]{3,2,1,0:T(8,128)S(1)} copy-done((f32[3,8,16,128]{3,2,1,0:T(8,128)S(1)}, f32[3,8,16,128]{3,2,1,0:T(8,128)}, u32[]{:S(2)}) %copy-start) | copy-done | bytes 196632
  1.6 0.0 copy-start.1
  1.6 0.8 %copy-done.1 = f32[8,16,128]{2,1,0:T(8,128)S(1)} copy-done((f32[8,16,128]{2,1,0:T(8,128)S(1)}, f32[8,16,128]{2,1,0:T(8,128)}, u32[]{:S(2)}) %copy-start.1) | copy-done | bytes 65560
  2.4 74.6 %shard_map.41 = (f32[3,8,16,128]{3,2,1,0:T(8,128)S(1)}, f32[3,8,16,128]{3,2,1,0:T(8,128)S(1)}) custom-call(f32[3,8,16,128]{3,2,1,0:T(8,128)S(1)} %copy-done, f32[8,16,128]{2,1,0:T(8,128)S(1)} %copy-done.1), custom_call_target="tpu_custom_call" | custom-call | tf_op jit(solution)/shard_map/pallas_call | solution.py:337
  77.0 0.7 copy.6
  77.7 0.7 copy.7
Async XLA Ops:
  0.6 0.9 %copy-start = (f32[3,8,16,128]{3,2,1,0:T(8,128)S(1)}, f32[3,8,16,128]{3,2,1,0:T(8,128)}, u32[]{:S(2)}) copy-start(f32[3,8,16,128]{3,2,1,0:T(8,128)} %f_ref.1) | copy-start | bytes 589828
  1.6 0.8 %copy-start.1 = (f32[8,16,128]{2,1,0:T(8,128)S(1)}, f32[8,16,128]{2,1,0:T(8,128)}, u32[]{:S(2)}) copy-start(f32[8,16,128]{2,1,0:T(8,128)} %v_ref.1) | copy-start | bytes 196612

commit v2 on v1

v2 whole, which is shorter than its diff:
```python
import functools
import jax
import jax.numpy as jnp
from jax import lax
from jax.experimental import pallas as pl
from jax.experimental.pallas import tpu as pltpu
from jax.sharding import PartitionSpec as P

ITERS = 3
AXES = ("gx", "gy", "gz")
MESH = pl.DeviceIdType.MESH
relax = 2.0 / 3.0
ROUNDS = 3 + 3 * ITERS
BESIDE = [(0, 0), (0, 1), (1, 0), (1, 1)]


def kernel(sizes, f_ref, v_ref, x_out, r_out, sx, sy, sz, sxy, syz, rx, ry, rz, rxy, ryz, rxz,
           cfE, cfY, cfZ, fwE, fwY, fwZ, ccE, ccY, ccZ, cwE, cwY, cwZ,
           ssend, srecv, red_src, red_dst, rsend, rrecv):
    NC, X, Y, Z = f_ref.shape
    T = Y // 8
    C = range(NC)
    place = [lax.axis_index(a) for a in AXES]
    total = [sizes[a] for a in AXES]
    gx_n, gy_n, gz_n = total
    plane = [(i, j) for i in range(gx_n) for j in range(gz_n) if (i, j) != (0, 0)]

    def plane_peer(i, j):
        return {"gx": lax.rem(place[0] + i, gx_n), "gz": lax.rem(place[2] + j, gz_n)}

    def line_peer(i):
        return {"gy": lax.rem(place[1] + i, gy_n)}

    def exists(offset):
        ok = None
        for a in range(3):
            if offset[a]:
                here = place[a] < total[a] - 1 if offset[a] > 0 else place[a] > 0
                ok = here if ok is None else jnp.logical_and(ok, here)
        return ok

    def peer_at(offset):
        return {AXES[a]: place[a] + offset[a] for a in range(3) if offset[a]}

    def side(up):
        return 1 if up else -1

    faces = [tuple(side(up) if a == b else 0 for b in range(3)) for a in range(3) for up in (0, 1)]
    pairs = ((0, 1), (1, 2), (0, 2))
    edges = [(pair_, i, j) for pair_ in pairs for i, j in BESIDE]

    def edge_offset(edge):
        (a, b), i, j = edge
        return tuple(side(i) if d == a else side(j) if d == b else 0 for d in range(3))

    barrier = pltpu.get_barrier_semaphore()
    for i, j in plane:
        pl.semaphore_signal(barrier, inc=1, device_id=plane_peer(i, j), device_id_type=MESH)
    for i in range(1, gy_n):
        pl.semaphore_signal(barrier, inc=1, device_id=line_peer(i), device_id_type=MESH)
    count = len(plane) + gy_n - 1
    for edge in edges:
        if edge[0] != (0, 2):
            ok, to = exists(edge_offset(edge)), peer_at(edge_offset(edge))

            @pl.when(ok)
            def _():
                pl.semaphore_signal(barrier, inc=1, device_id=to, device_id_type=MESH)

            count = count + ok.astype(jnp.int32)

    for a, buf in enumerate((rx, ry, rz)):
        for up in (0, 1):
            @pl.when(jnp.logical_not(exists(faces[2 * a + up])))
            def _():
                buf[:, up] = jnp.zeros_like(buf[:, up])
    for n, buf in enumerate((rxy, ryz, rxz)):
        for e in range(4):
            @pl.when(jnp.logical_not(exists(edge_offset(edges[4 * n + e]))))
            def _():
                buf[:, e] = jnp.zeros_like(buf[:, e])

    lane = lax.broadcasted_iota(jnp.int32, (8, Z), 1)
    sub = lax.broadcasted_iota(jnp.int32, (8, Z), 0)
    iy = lax.broadcasted_iota(jnp.int32, (1, Y, Z), 1)
    iz = lax.broadcasted_iota(jnp.int32, (1, Y, Z), 2)

    def copies(slot, nc, nx):
        fine = nx == X
        planes = 2 * nc if fine else 2
        rows_n = 2 * nc
        made = []

        def make(n, offset, src, dst, mine, opposite):
            made.append((n, exists(offset),
                pltpu.make_async_remote_copy(
                    src_ref=src, dst_ref=dst, send_sem=ssend.at[slot, n],
                    recv_sem=srecv.at[slot, opposite], device_id=peer_at(offset), device_id_type=MESH),
                pltpu.make_async_remote_copy(
                    src_ref=src, dst_ref=mine, send_sem=ssend.at[slot, n],
                    recv_sem=srecv.at[slot, n], device_id=peer_at(offset), device_id_type=MESH)))

        for n, offset in enumerate(faces):
            a, up = n // 2, n % 2
            if a == 0:
                cut = pl.ds(0, planes)
                make(n, offset, sx.at[slot, up, cut], rx.at[slot, 1 - up, cut], rx.at[slot, up, cut], n ^ 1)
            elif a == 1:
                cut = pl.ds(0, rows_n)
                make(n, offset, sy.at[slot, up, cut], ry.at[slot, 1 - up, cut], ry.at[slot, up, cut], n ^ 1)
            else:
                make(n, offset, sz.at[slot], rz.at[slot, 1 - up], rz.at[slot, up], n ^ 1)
        for m, edge in enumerate(edges):
            pair_, i, j = edge
            e, far = 2 * i + j, 2 * (1 - i) + (1 - j)
            n, opposite = 6 + m, 6 + 4 * (m // 4) + far
            if pair_ == (0, 1):
                src, dst = sxy.at[slot, e], rxy
            elif pair_ == (1, 2):
                src, dst = syz.at[slot, i], ryz
            else:
                src, dst = sz.at[slot], rxz
            make(n, edge_offset(edge), src, dst.at[slot, far], dst.at[slot, e], opposite)
        return made

    used = []

    def go(made, which):
        for n, ok, copy, _ in made:
            if n in which:
                pl.when(ok)(copy.start)

    def launch(slot, comps, unit):
        nc, nx = len(comps), comps[0].shape[0]
        used.append((slot, nc, nx))
        made = copies(slot, nc, nx)
        for up in (0, 1):
            for layer in (0, 1):
                k = nx - 1 - layer if up else layer
                if nx == X:
                    for c in range(nc):
                        sx[slot, up, layer * nc + c] = comps[c][k]
                else:
                    flat = comps[0][k]
                    if nc > 1:
                        flat = jnp.where(iy[0] % 2 == 1, comps[1][k], flat)
                    if nc > 2:
                        flat = jnp.where(iz[0] % 2 == 1, comps[2][k], flat)
                    sx[slot, up, layer] = flat
        go(made, (0, 1))
        for up in (0, 1):
            for c, v in enumerate(comps):
                for i in range(X):
                    k = i * nx // X
                    for layer in (0, 1):
                        row = Y - 1 - layer * unit if up else layer * unit
                        sy[slot, up, layer * nc + c, i : i + 1] = v[k, row : row + 1]
                    if i in (0, X - 1):
                        sxy[slot, (2 if i else 0) + up, c : c + 1] = v[k, Y - 1 if up else 0][None]
        go(made, (2, 3, 6, 7, 8, 9))
        wide = 4 * unit
        for t in range(T):
            packed = jnp.zeros((8, Z), jnp.float32)
            for c, v in enumerate(comps):
                for i in range(nx):
                    at = wide * (c * nx + i)
                    rolled = pltpu.roll(v[i, 8 * t : 8 * t + 8], (at + 2 * unit) % Z, 1)
                    packed = jnp.where(lane >= at, rolled, packed)
            sz[slot, t] = packed
        go(made, (4, 5, 14, 15, 16, 17))
        for up in (0, 1):
            packed = jnp.zeros((8, Z), jnp.float32)
            for c in range(nc):
                at = wide * c * nx
                rolled = pltpu.roll(sy[slot, up, c], (at + 2 * unit) % Z, 1)
                packed = jnp.where(lane >= at, rolled, packed)
            syz[slot, up] = packed
        go(made, (10, 11, 12, 13))

    def rot(v, amount, axis):
        amount = amount % v.shape[axis]
        return pltpu.roll(v, amount, axis) if amount else v

    def near(below, above, unit):
        return jnp.where(lane % (4 * unit) < unit, rot(above, -2 * unit, 1), below)

    def unpack(tile, k, unit):
        return rot(tile, -unit - 4 * unit * k, 1)

    def stack(parts):
        return jnp.concatenate([q_[None] for q_ in parts], axis=0)

    def column(tiles, k, unit):
        return jnp.concatenate([unpack(tile, k, unit) for tile in tiles], axis=0)

    def six(v, hxm, hxp, hym, hyp, hz, unit):
        return (
            jnp.concatenate([v[1:], hxp[None]], axis=0),
            jnp.concatenate([hxm[None], v[:-1]], axis=0),
            jnp.where(iy >= Y - unit, hyp, pltpu.roll(v, Y - unit, 1)),
            jnp.where(iy < unit, hym, pltpu.roll(v, unit, 1)),
            jnp.where(iz >= Z - unit, hz, pltpu.roll(v, Z - unit, 2)),
            jnp.where(iz < unit, hz, pltpu.roll(v, unit, 2)),
        )

    def slab_rows(slab, nx):
        return [slab[i * X // nx : i * X // nx + 1] for i in range(nx)]

    def expand(flat, c):
        odd_z = iz[0] % 2 == 1
        odd_y = iy[0] % 2 == 1
        v = jnp.where(odd_z, flat, rot(flat, -1, 1)) if c == 2 else jnp.where(odd_z, rot(flat, 1, 1), flat)
        return jnp.where(odd_y, v, rot(v, -1, 0)) if c == 1 else jnp.where(odd_y, rot(v, 1, 0), v)

    def land(slot, comps, unit):
        nc, nx = len(comps), comps[0].shape[0]
        for n, ok, _, arrive in copies(slot, nc, nx):
            pl.when(ok)(arrive.wait_recv)
        wide = 4 * unit

        def xplane(c, up, layer):
            if nx == X:
                return rx[slot, up, layer * nc + c]
            flat = rx[slot, up, layer]
            if nc == 1:
                return flat
            return expand(flat, c)

        H1 = [near(rz[slot, 0, t], rz[slot, 1, t], unit) for t in range(T)]
        H2 = [jnp.where(lane % wide < unit, rot(rz[slot, 1, t], -3 * unit, 1), rot(rz[slot, 0, t], unit, 1))
              for t in range(T)]
        EX = [[near(rxz[slot, 2 * a, t], rxz[slot, 2 * a + 1, t], unit) for t in range(T)] for a in (0, 1)]
        EY = [near(ryz[slot, 2 * b], ryz[slot, 2 * b + 1], unit) for b in (0, 1)]
        field = {"E": [], "Y": [], "Z": H1}
        nbs = {"E": [], "Y": [], "Z": []}
        ux = X // nx
        for c, v in enumerate(comps):
            ext = jnp.concatenate([xplane(c, 0, 0)[None], v, xplane(c, 1, 0)[None]], axis=0)
            hy = []
            for b in (0, 1):
                hy.append(stack([rxy[slot, b, c : c + 1]] + slab_rows(ry[slot, b, c], nx) + [rxy[slot, 2 + b, c : c + 1]]))
            hz = stack([column(EX[0], c * nx + nx - 1, unit)] + [column(H1, c * nx + i, unit) for i in range(nx)]
                       + [column(EX[1], c * nx, unit)])
            field["E"].append(ext)
            nbs["E"].append(six(ext, xplane(c, 0, 1), xplane(c, 1, 1), hy[0], hy[1], hz, unit))
            fy, ny = [], []
            for b in (0, 1):
                slab = ry[slot, b, c]
                out, inner = ry[slot, b, nc + c], sy[slot, b, c]
                hzs = unpack(EY[b], c * nx, unit)
                fy.append(slab)
                ny.append((
                    jnp.where(sub >= 8 - ux, rxy[slot, 2 + b, c : c + 1], rot(slab, -ux, 0)),
                    jnp.where(sub < ux, rxy[slot, b, c : c + 1], rot(slab, ux, 0)),
                    out, inner,
                    jnp.where(lane >= Z - unit, hzs, rot(slab, -unit, 1)),
                    jnp.where(lane < unit, hzs, rot(slab, unit, 1)),
                ))
            field["Y"].append(fy)
            nbs["Y"].append(ny)
        which = lane // wide % nx
        rim = []
        for b in (0, 1):
            line = jnp.zeros((1, Z), jnp.float32)
            for i in range(nx):
                row = EY[b][i * ux : i * ux + 1]
                line = jnp.where(which[0:1] == i, rot(row, wide * i, 1), line)
            rim.append(line)
        for t in range(T):
            h = H1[t]
            before = rim[0] if t == 0 else rot(H1[t - 1], unit, 0)
            after = rim[1] if t == T - 1 else rot(H1[t + 1], -unit, 0)
            nbs["Z"].append((
                jnp.where(which == nx - 1, rot(EX[1][t], wide * (nx - 1), 1), rot(h, -wide, 1)),
                jnp.where(which == 0, rot(EX[0][t], -wide * (nx - 1), 1), rot(h, wide, 1)),
                jnp.where(sub >= 8 - unit, after, rot(h, -unit, 0)),
                jnp.where(sub < unit, before, rot(h, unit, 0)),
                H2[t],
                rot(sz[slot, t], -unit, 1),
            ))
        return field, nbs

    def stencil(v, nb, coef, mass):
        out = v * mass if mass != 1.0 else v
        for d in range(6):
            out = out + coef[d] * (v - nb[d])
        return out

    def viscous_wide(field, nbs, coefs, mass):
        cE, cY, cZ = coefs
        return {
            "E": [stencil(v, nb, cE, mass) for v, nb in zip(field["E"], nbs["E"])],
            "Y": [[stencil(f[b], n[b], cY[b], mass) for b in (0, 1)] for f, n in zip(field["Y"], nbs["Y"])],
            "Z": [stencil(field["Z"][t], nbs["Z"][t], [cZ[d, t] for d in range(6)], mass) for t in range(T)],
        }

    def viscous(field, coefs, mass, unit):
        out = []
        for c in C:
            ext = field["E"][c]
            nx = ext.shape[0] - 2
            hy = [stack(slab_rows(field["Y"][c][b], nx)) for b in (0, 1)]
            hz = stack([column(field["Z"], c * nx + i, unit) for i in range(nx)])
            v = ext[1 : nx + 1]
            nb = six(v, ext[0], ext[nx + 1], hy[0], hy[1], hz, unit)
            out.append(stencil(v, nb, [coefs[0][d, 1 : nx + 1] for d in range(6)], mass))
        return out

    def fmap(fn, *fields):
        return {
            "E": [fn(*parts) for parts in zip(*(f["E"] for f in fields))],
            "Y": [[fn(*(f["Y"][c][b] for f in fields)) for b in (0, 1)] for c in range(len(fields[0]["Y"]))],
            "Z": [fn(*parts) for parts in zip(*(f["Z"] for f in fields))],
        }

    def flat_row(scalar, like):
        return scalar if like.ndim == 3 else scalar[0]

    def weights(E, Yw, Zw):
        return {"E": [E[...]] * NC, "Y": [[Yw[b] for b in (0, 1)]] * NC, "Z": [Zw[t] for t in range(T)]}

    def core(field):
        return [e[1 : e.shape[0] - 1] for e in field["E"]]

    def pairsum(v):
        v = v.reshape(X // 2, 2, Y, Z)
        v = v[:, 0] + v[:, 1]
        v = v + jnp.where(iy % 2 == 0, pltpu.roll(v, Y - 1, 1), pltpu.roll(v, 1, 1))
        return v + jnp.where(iz % 2 == 0, pltpu.roll(v, Z - 1, 2), pltpu.roll(v, 1, 2))

    def prolong(field):
        def deep(e):
            n = e.shape[0] - 2
            return jnp.concatenate([e[0:1]] + [e[1 + i : 2 + i] for i in range(n) for _ in (0, 1)] + [e[n + 1 :]], axis=0)

        def thin(h):
            m = lane % 8
            return jnp.where(m == 0, h, jnp.where(m == 1, rot(h, -1, 1), jnp.where(m == 4, rot(h, 4, 1), rot(h, 3, 1))))

        return {"E": [deep(e) for e in field["E"]], "Y": field["Y"], "Z": [thin(h) for h in field["Z"]]}

    inside = [jnp.where(exists(f), 1.0, 0.0).astype(jnp.float32) for f in faces]

    def set_up(field, nbs, nx, unit, mass, scale, E, Yc, Zc, wE, wY, wZ):
        v = field["E"][0]
        ix = lax.broadcasted_iota(jnp.int32, v.shape, 0)
        keep = jnp.where(ix == 0, inside[0], jnp.where(ix == nx + 1, inside[1], 1.0))
        diag = jnp.full(v.shape, mass, jnp.float32)
        for d in range(6):
            face = scale * (v + nbs["E"][0][d]) * keep
            E[d] = face
            diag = diag + face
        wE[...] = relax / diag
        for b in (0, 1):
            v = field["Y"][0][b]
            diag = jnp.full(v.shape, mass, jnp.float32)
            for d in range(6):
                face = scale * (v + nbs["Y"][0][b][d]) * inside[2 + b]
                Yc[b, d] = face
                diag = diag + face
            wY[b] = relax / diag
        keep = jnp.where(lane % (4 * unit) < unit, inside[5], inside[4])
        span = 4 * unit * nx
        for t in range(T):
            v = field["Z"][t]
            diag = jnp.full(v.shape, mass, jnp.float32)
            for d in range(6):
                face = scale * (v + nbs["Z"][t][d]) * keep
                each = face
                for c in range(1, NC):
                    each = jnp.where(lane >= c * span, rot(face, c * span, 1), each)
                Zc[d, t] = each
                diag = diag + each
            wZ[t] = relax / diag

    fine = (cfE, cfY, cfZ)
    coarse = (ccE, ccY, ccZ)
    visc = v_ref[...]
    cvisc = pairsum(visc) * 0.125
    force = [f_ref[c] for c in C]
    pl.semaphore_wait(barrier, count)
    launch(0, [visc], 1)
    launch(1, force, 1)
    launch(2, [cvisc], 2)
    field, nbs = land(0, [visc], 1)
    set_up(field, nbs, X, 1, 1.0, 0.5, cfE, cfY, cfZ, fwE, fwY, fwZ)
    field, nbs = land(2, [cvisc], 2)
    set_up(field, nbs, X // 2, 2, 8.0, 2.0, ccE, ccY, ccZ, cwE, cwY, cwZ)
    forced, _ = land(1, force, 1)
    next_slot = [3]

    def take():
        next_slot[0] += 1
        return next_slot[0] - 1

    def pair(vec, middle):
        fw = weights(fwE, fwY, fwZ)
        cw = weights(cwE, cwY, cwZ)
        nxc = X // 2
        sm = fmap(lambda a, b: a * b, vec, fw)
        applied = viscous(sm, fine, 1.0, 1)
        cwl = cwE[1 : nxc + 1]
        local = core(vec)
        first = [cwl * pairsum(local[c] - applied[c]) for c in C]
        slot = take()
        launch(slot, first, 2)
        one, nbs = land(slot, first, 2)
        two = fmap(lambda a, b, k: a + a - k * b, one, viscous_wide(one, nbs, coarse, 8.0), cw)
        applied = viscous(two, coarse, 8.0, 2)
        three = [v + first[c] - cwl * applied[c] for c, v in enumerate(core(two))]
        slot = take()
        launch(slot, three, 2)
        middle()
        field, nbs = land(slot, three, 2)
        four = fmap(lambda a, o, b, k: a + o - k * b, field, one, viscous_wide(field, nbs, coarse, 8.0), cw)
        sm = fmap(lambda a, b: a + b, sm, prolong(four))
        applied = viscous(sm, fine, 1.0, 1)
        fwl = fwE[1 : X + 1]
        m = [v + fwl * (local[c] - applied[c]) for c, v in enumerate(core(sm))]
        slot = take()
        launch(slot, m, 1)
        field, nbs = land(slot, m, 1)
        return m, viscous_wide(field, nbs, fine, 1.0)

    def red_copy(n, stage, k):
        if stage == 0:
            i, j = plane[k]
            peer, base = plane_peer(i, j), k
        else:
            peer, base = line_peer(k + 1), len(plane) + k
        return pltpu.make_async_remote_copy(
            src_ref=red_src.at[n, stage], dst_ref=red_dst.at[n, base],
            send_sem=rsend.at[n, base], recv_sem=rrecv.at[n, base],
            device_id=peer, device_id_type=MESH)

    def peers(stage):
        return range(len(plane)) if stage == 0 else range(gy_n - 1)

    def fold(v):
        v = v.reshape(X * T, 8, Z).sum(axis=0)
        return v + pltpu.roll(v, 4, 0)

    def reduce_start(n, r, u, w):
        g = d = 0.0
        for c in C:
            g = g + r[c] * u[c]
            d = d + u[c] * w[c]
        red_src[n, 0] = jnp.where(sub < 4, fold(g), fold(d))
        for k in peers(0):
            red_copy(n, 0, k).start()

    def reduce_middle(n):
        acc = red_src[n, 0]
        for k in peers(0):
            red_copy(n, 0, k).wait_recv()
            acc = acc + red_dst[n, k]
        red_src[n, 1] = acc
        for k in peers(1):
            red_copy(n, 1, k).start()

    def reduce_end(n):
        acc = red_src[n, 1]
        for k in peers(1):
            red_copy(n, 1, k).wait_recv()
            acc = acc + red_dst[n, len(plane) + k]
        g = jnp.sum(jnp.where(sub < 4, acc, 0.0))
        d = jnp.sum(jnp.where(sub < 4, 0.0, acc))
        return jnp.full((1, 1, Z), g), jnp.full((1, 1, Z), d)

    u, w = pair(forced, lambda: None)
    r = force
    gamma_old = alpha_old = None
    for n in range(ITERS):
        last = n == ITERS - 1
        wl = core(w)
        reduce_start(n, r, u, wl)
        if last:
            reduce_middle(n)
        else:
            m, nn = pair(w, lambda: reduce_middle(n))
        gamma, delta = reduce_end(n)
        if n == 0:
            alpha = gamma / delta
            p, s = u, wl
        else:
            beta = gamma / gamma_old
            alpha = gamma / (delta - beta * gamma / alpha_old)
            p = [u[c] + beta * p[c] for c in C]
            s = [wl[c] + beta * s[c] for c in C]
        for c in C:
            x_out[c] = alpha * p[c] if n == 0 else x_out[c] + alpha * p[c]
        r = [r[c] - alpha * s[c] for c in C]
        if last:
            for c in C:
                r_out[c] = r[c]
            break
        if n == 0:
            q, z = m, nn
        else:
            q = [m[c] + beta * q[c] for c in C]
            z = fmap(lambda a, b: a + flat_row(beta, a) * b, nn, z)
        u = [u[c] - alpha * q[c] for c in C]
        w = fmap(lambda a, b: a - flat_row(alpha, a) * b, w, z)
        gamma_old, alpha_old = gamma, alpha

    for slot, nc, nx in used:
        for _, ok, copy, _ in copies(slot, nc, nx):
            pl.when(ok)(copy.wait_send)
    for n in range(ITERS):
        for stage in (0, 1):
            for k in peers(stage):
                red_copy(n, stage, k).wait_send()


def solution(mesh):
    sizes = dict(mesh.shape)

    def shards(forcing, viscosity):
        NC, X, Y, Z = forcing.shape
        T = Y // 8
        f32 = jnp.float32
        peers = sizes["gx"] * sizes["gz"] - 1 + sizes["gy"] - 1
        spec = pl.BlockSpec(memory_space=pltpu.VMEM)
        out = jax.ShapeDtypeStruct(forcing.shape, f32)
        dma = pltpu.SemaphoreType.DMA
        V = lambda *shape: pltpu.VMEM(shape, f32)
        coefs = lambda nx: [V(6, nx + 2, Y, Z), V(2, 6, 8, Z), V(6, T, 8, Z)]
        weights = lambda nx: [V(nx + 2, Y, Z), V(2, 8, Z), V(T, 8, Z)]
        halo = [V(ROUNDS, 2, 2 * NC, Y, Z), V(ROUNDS, 2, 2 * NC, 8, Z)]
        return pl.pallas_call(
            functools.partial(kernel, sizes),
            out_shape=(out, out),
            in_specs=[spec, spec],
            out_specs=(spec, spec),
            scratch_shapes=halo + [V(ROUNDS, T, 8, Z), V(ROUNDS, 4, 8, Z), V(ROUNDS, 2, 8, Z)]
            + halo + [V(ROUNDS, 2, T, 8, Z), V(ROUNDS, 4, 8, Z), V(ROUNDS, 4, 8, Z), V(ROUNDS, 4, T, 8, Z)]
            + coefs(X) + weights(X) + coefs(X // 2) + weights(X // 2) + [
                dma((ROUNDS, 18)),
                dma((ROUNDS, 18)),
                V(ITERS, 2, 8, Z),
                V(ITERS, peers, 8, Z),
                dma((ITERS, peers)),
                dma((ITERS, peers)),
            ],
            compiler_params=pltpu.CompilerParams(
                collective_id=0, has_side_effects=True, vmem_limit_bytes=48 * 1024 * 1024
            ),
        )(forcing, viscosity)

    return jax.shard_map(
        shards,
        mesh=mesh,
        in_specs=(P(None, "gx", "gy", "gz"), P("gx", "gy", "gz")),
        out_specs=(P(None, "gx", "gy", "gz"), P(None, "gx", "gy", "gz")),
        check_vma=False,
    )
```

time: 78.6 us -> 61.8 us (0.79)
  Pallas kernels: 74.6 us -> 57.9 us
    pallas_call x1, Pallas kernels: 74.6 us -> 57.9 us  [shards(): pl.pallas_call(functools.partial(kernel, sizes), out_shape=(out, out), in...]
where the time goes in v2:
time: 61.8 us; the launch traced here: 61.7 us
  Pallas kernels  57.9 us (94%)
  local copies, waits for them, and re-layouts  3.11 us (5%)
  between operations  0.65 us (1%)
    pallas_call x1, Pallas kernels, shards(): pl.pallas_call(functools.partial(kernel, sizes), out_shape=(out, out), in...  57.9 us
    unnamed x6, local copies, waits for them, and re-layouts  3.11 us

profile of v2, /device:TPU:0, one launch (start us, length us, event | category | flops | bytes accessed | tf_op | source)
XLA Modules:
  0.0 61.7 jit_solution(14954278061369132135)
XLA Ops:
  0.6 0.0 copy-start
  0.6 0.9 %copy-done = f32[3,8,16,128]{3,2,1,0:T(8,128)S(1)} copy-done((f32[3,8,16,128]{3,2,1,0:T(8,128)S(1)}, f32[3,8,16,128]{3,2,1,0:T(8,128)}, u32[]{:S(2)}) %copy-start) | copy-done | bytes 196632
  1.6 0.0 copy-start.1
  1.6 0.8 %copy-done.1 = f32[8,16,128]{2,1,0:T(8,128)S(1)} copy-done((f32[8,16,128]{2,1,0:T(8,128)S(1)}, f32[8,16,128]{2,1,0:T(8,128)}, u32[]{:S(2)}) %copy-start.1) | copy-done | bytes 65560
  2.4 57.9 %shard_map.41 = (f32[3,8,16,128]{3,2,1,0:T(8,128)S(1)}, f32[3,8,16,128]{3,2,1,0:T(8,128)S(1)}) custom-call(f32[3,8,16,128]{3,2,1,0:T(8,128)S(1)} %copy-done, f32[8,16,128]{2,1,0:T(8,128)S(1)} %copy-done.1), custom_call_target="tpu_custom_call" | custom-call | tf_op jit(solution)/shard_map/pallas_call | solution.py:530
  60.3 0.7 %copy.6 = f32[3,8,16,128]{3,2,1,0:T(8,128)} copy(f32[3,8,16,128]{3,2,1,0:T(8,128)S(1)} %get-tuple-element.4) | data formatting | bytes 393216
  61.0 0.7 %copy.7 = f32[3,8,16,128]{3,2,1,0:T(8,128)} copy(f32[3,8,16,128]{3,2,1,0:T(8,128)S(1)} %get-tuple-element.5) | data formatting | bytes 393216
Async XLA Ops:
  0.6 0.9 %copy-start = (f32[3,8,16,128]{3,2,1,0:T(8,128)S(1)}, f32[3,8,16,128]{3,2,1,0:T(8,128)}, u32[]{:S(2)}) copy-start(f32[3,8,16,128]{3,2,1,0:T(8,128)} %f_ref.1) | copy-start | bytes 589828
  1.6 0.8 %copy-start.1 = (f32[8,16,128]{2,1,0:T(8,128)S(1)}, f32[8,16,128]{2,1,0:T(8,128)}, u32[]{:S(2)}) copy-start(f32[8,16,128]{2,1,0:T(8,128)} %v_ref.1) | copy-start | bytes 196612

commit v3 on v2

--- a/solution.py
+++ b/solution.py
@@ -15,7 +15,7 @@
 
 
 def kernel(sizes, f_ref, v_ref, x_out, r_out, sx, sy, sz, sxy, syz, rx, ry, rz, rxy, ryz, rxz,
-           cfE, cfY, cfZ, fwE, fwY, fwZ, ccE, ccY, ccZ, cwE, cwY, cwZ,
+           cfE, cfY, cfZ, fwE, fwY, fwZ, ccE, ccY, ccZ, cwE, cwY, cwZ, fin, frim, cin, crim,
            ssend, srecv, red_src, red_dst, rsend, rrecv):
     NC, X, Y, Z = f_ref.shape
     T = Y // 8
@@ -126,9 +126,8 @@
     used = []
 
     def go(made, which):
-        for n, ok, copy, _ in made:
-            if n in which:
-                pl.when(ok)(copy.start)
+        for n in which:
+            pl.when(made[n][1])(made[n][2].start)
 
     def launch(slot, comps, unit):
         nc, nx = len(comps), comps[0].shape[0]
@@ -147,7 +146,6 @@
                     if nc > 2:
                         flat = jnp.where(iz[0] % 2 == 1, comps[2][k], flat)
                     sx[slot, up, layer] = flat
-        go(made, (0, 1))
         for up in (0, 1):
             for c, v in enumerate(comps):
                 for i in range(X):
@@ -157,8 +155,17 @@
                         sy[slot, up, layer * nc + c, i : i + 1] = v[k, row : row + 1]
                     if i in (0, X - 1):
                         sxy[slot, (2 if i else 0) + up, c : c + 1] = v[k, Y - 1 if up else 0][None]
-        go(made, (2, 3, 6, 7, 8, 9))
         wide = 4 * unit
+        go(made, (6, 7, 8, 9))
+        for up in (0, 1):
+            packed = jnp.zeros((8, Z), jnp.float32)
+            for c in range(nc):
+                at = wide * c * nx
+                rolled = pltpu.roll(sy[slot, up, c], (at + 2 * unit) % Z, 1)
+                packed = jnp.where(lane >= at, rolled, packed)
+            syz[slot, up] = packed
+        go(made, (10, 11, 12, 13))
+        go(made, (2, 3))
         for t in range(T):
             packed = jnp.zeros((8, Z), jnp.float32)
             for c, v in enumerate(comps):
@@ -167,15 +174,7 @@
                     rolled = pltpu.roll(v[i, 8 * t : 8 * t + 8], (at + 2 * unit) % Z, 1)
                     packed = jnp.where(lane >= at, rolled, packed)
             sz[slot, t] = packed
-        go(made, (4, 5, 14, 15, 16, 17))
-        for up in (0, 1):
-            packed = jnp.zeros((8, Z), jnp.float32)
-            for c in range(nc):
-                at = wide * c * nx
-                rolled = pltpu.roll(sy[slot, up, c], (at + 2 * unit) % Z, 1)
-                packed = jnp.where(lane >= at, rolled, packed)
-            syz[slot, up] = packed
-        go(made, (10, 11, 12, 13))
+        go(made, (14, 15, 16, 17, 0, 1, 4, 5))
 
     def rot(v, amount, axis):
         amount = amount % v.shape[axis]
@@ -212,7 +211,43 @@
         v = jnp.where(odd_z, flat, rot(flat, -1, 1)) if c == 2 else jnp.where(odd_z, rot(flat, 1, 1), flat)
         return jnp.where(odd_y, v, rot(v, -1, 0)) if c == 1 else jnp.where(odd_y, rot(v, 1, 0), v)
 
-    def land(slot, comps, unit):
+    def partial(v, coefs, extra, mass, unit):
+        nx = v.shape[0]
+        inn = extra[0]
+        out = v * mass if mass != 1.0 else v
+        out = out + inn[0] * (v - pltpu.roll(v, Y - unit, 1))
+        out = out + inn[1] * (v - pltpu.roll(v, unit, 1))
+        out = out + inn[2] * (v - pltpu.roll(v, Z - unit, 2))
+        out = out + inn[3] * (v - pltpu.roll(v, unit, 2))
+        flow = coefs[0][0, 1:nx] * (v[:-1] - v[1:])
+        none = jnp.zeros((1, Y, Z), jnp.float32)
+        return out + jnp.concatenate([flow, none], axis=0) - jnp.concatenate([none, flow], axis=0)
+
+    def finish(ext, far_below, far_above, hy, hz, part, coefs, extra, mass, unit):
+        nx = ext.shape[0] - 2
+        v = ext[1 : nx + 1]
+        cE, rim = coefs[0], extra[1]
+        out = part + rim[1] * (v - hz[1 : nx + 1])
+        out = out + rim[0] * (v - jnp.where(iy < Y // 2, hy[0][1 : nx + 1], hy[1][1 : nx + 1]))
+        first = out[0:1] + cE[1, 1:2] * (v[0:1] - ext[0:1])
+        final = out[nx - 1 :] + cE[0, nx : nx + 1] * (v[nx - 1 :] - ext[nx + 1 :])
+
+        def sheet(k, beyond, before):
+            e, h = ext[k : k + 1], hz[k : k + 1]
+            nb = (
+                beyond, before,
+                jnp.where(iy >= Y - unit, hy[1][k : k + 1], pltpu.roll(e, Y - unit, 1)),
+                jnp.where(iy < unit, hy[0][k : k + 1], pltpu.roll(e, unit, 1)),
+                jnp.where(iz >= Z - unit, h, pltpu.roll(e, Z - unit, 2)),
+                jnp.where(iz < unit, h, pltpu.roll(e, unit, 2)),
+            )
+            return stencil(e, nb, [cE[d, k : k + 1] for d in range(6)], mass)
+
+        low = sheet(0, v[0:1], far_below[None])
+        high = sheet(nx + 1, far_above[None], v[nx - 1 :])
+        return jnp.concatenate([low, first, out[1 : nx - 1], final, high], axis=0)
+
+    def land(slot, comps, unit, parts=None, work=None):
         nc, nx = len(comps), comps[0].shape[0]
         for n, ok, _, arrive in copies(slot, nc, nx):
             pl.when(ok)(arrive.wait_recv)
@@ -242,7 +277,10 @@
             hz = stack([column(EX[0], c * nx + nx - 1, unit)] + [column(H1, c * nx + i, unit) for i in range(nx)]
                        + [column(EX[1], c * nx, unit)])
             field["E"].append(ext)
-            nbs["E"].append(six(ext, xplane(c, 0, 1), xplane(c, 1, 1), hy[0], hy[1], hz, unit))
+            if parts is None:
+                nbs["E"].append(six(ext, xplane(c, 0, 1), xplane(c, 1, 1), hy[0], hy[1], hz, unit))
+            else:
+                nbs["E"].append(finish(ext, xplane(c, 0, 1), xplane(c, 1, 1), hy, hz, parts[c], *work, unit))
             fy, ny = [], []
             for b in (0, 1):
                 slab = ry[slot, b, c]
@@ -289,7 +327,7 @@
     def viscous_wide(field, nbs, coefs, mass):
         cE, cY, cZ = coefs
         return {
-            "E": [stencil(v, nb, cE, mass) for v, nb in zip(field["E"], nbs["E"])],
+            "E": nbs["E"],
             "Y": [[stencil(f[b], n[b], cY[b], mass) for b in (0, 1)] for f, n in zip(field["Y"], nbs["Y"])],
             "Z": [stencil(field["Z"][t], nbs["Z"][t], [cZ[d, t] for d in range(6)], mass) for t in range(T)],
         }
@@ -341,7 +379,7 @@
 
     inside = [jnp.where(exists(f), 1.0, 0.0).astype(jnp.float32) for f in faces]
 
-    def set_up(field, nbs, nx, unit, mass, scale, E, Yc, Zc, wE, wY, wZ):
+    def set_up(field, nbs, nx, unit, mass, scale, E, Yc, Zc, wE, wY, wZ, extra):
         v = field["E"][0]
         ix = lax.broadcasted_iota(jnp.int32, v.shape, 0)
         keep = jnp.where(ix == 0, inside[0], jnp.where(ix == nx + 1, inside[1], 1.0))
@@ -351,6 +389,14 @@
             E[d] = face
             diag = diag + face
         wE[...] = relax / diag
+        inn, rim = extra
+        c2, c3, c4, c5 = (E[d, 1 : nx + 1] for d in range(2, 6))
+        inn[0] = jnp.where(iy >= Y - unit, 0.0, c2)
+        inn[1] = jnp.where(iy < unit, 0.0, c3)
+        inn[2] = jnp.where(iz >= Z - unit, 0.0, c4)
+        inn[3] = jnp.where(iz < unit, 0.0, c5)
+        rim[0] = jnp.where(iy >= Y - unit, c2, jnp.where(iy < unit, c3, 0.0))
+        rim[1] = jnp.where(iz >= Z - unit, c4, jnp.where(iz < unit, c5, 0.0))
         for b in (0, 1):
             v = field["Y"][0][b]
             diag = jnp.full(v.shape, mass, jnp.float32)
@@ -383,9 +429,9 @@
     launch(1, force, 1)
     launch(2, [cvisc], 2)
     field, nbs = land(0, [visc], 1)
-    set_up(field, nbs, X, 1, 1.0, 0.5, cfE, cfY, cfZ, fwE, fwY, fwZ)
+    set_up(field, nbs, X, 1, 1.0, 0.5, cfE, cfY, cfZ, fwE, fwY, fwZ, (fin, frim))
     field, nbs = land(2, [cvisc], 2)
-    set_up(field, nbs, X // 2, 2, 8.0, 2.0, ccE, ccY, ccZ, cwE, cwY, cwZ)
+    set_up(field, nbs, X // 2, 2, 8.0, 2.0, ccE, ccY, ccZ, cwE, cwY, cwZ, (cin, crim))
     forced, _ = land(1, force, 1)
     next_slot = [3]
 
@@ -404,14 +450,16 @@
         first = [cwl * pairsum(local[c] - applied[c]) for c in C]
         slot = take()
         launch(slot, first, 2)
-        one, nbs = land(slot, first, 2)
+        parts = [partial(v, *(coarse, (cin, crim), 8.0), 2) for v in first]
+        one, nbs = land(slot, first, 2, parts, (coarse, (cin, crim), 8.0))
         two = fmap(lambda a, b, k: a + a - k * b, one, viscous_wide(one, nbs, coarse, 8.0), cw)
         applied = viscous(two, coarse, 8.0, 2)
         three = [v + first[c] - cwl * applied[c] for c, v in enumerate(core(two))]
         slot = take()
         launch(slot, three, 2)
+        parts = [partial(v, *(coarse, (cin, crim), 8.0), 2) for v in three]
         middle()
-        field, nbs = land(slot, three, 2)
+        field, nbs = land(slot, three, 2, parts, (coarse, (cin, crim), 8.0))
         four = fmap(lambda a, o, b, k: a + o - k * b, field, one, viscous_wide(field, nbs, coarse, 8.0), cw)
         sm = fmap(lambda a, b: a + b, sm, prolong(four))
         applied = viscous(sm, fine, 1.0, 1)
@@ -419,7 +467,8 @@
         m = [v + fwl * (local[c] - applied[c]) for c, v in enumerate(core(sm))]
         slot = take()
         launch(slot, m, 1)
-        field, nbs = land(slot, m, 1)
+        parts = [partial(v, *(fine, (fin, frim), 1.0), 1) for v in m]
+        field, nbs = land(slot, m, 1, parts, (fine, (fin, frim), 1.0))
         return m, viscous_wide(field, nbs, fine, 1.0)
 
     def red_copy(n, stage, k):
@@ -534,7 +583,8 @@
             out_specs=(spec, spec),
             scratch_shapes=halo + [V(ROUNDS, T, 8, Z), V(ROUNDS, 4, 8, Z), V(ROUNDS, 2, 8, Z)]
             + halo + [V(ROUNDS, 2, T, 8, Z), V(ROUNDS, 4, 8, Z), V(ROUNDS, 4, 8, Z), V(ROUNDS, 4, T, 8, Z)]
-            + coefs(X) + weights(X) + coefs(X // 2) + weights(X // 2) + [
+            + coefs(X) + weights(X) + coefs(X // 2) + weights(X // 2)
+            + [V(4, X, Y, Z), V(2, X, Y, Z), V(4, X // 2, Y, Z), V(2, X // 2, Y, Z)] + [
                 dma((ROUNDS, 18)),
                 dma((ROUNDS, 18)),
                 V(ITERS, 2, 8, Z),

time: 61.8 us -> 60.3 us (0.976)
  Pallas kernels: 57.9 us -> 56.3 us
    pallas_call x1, Pallas kernels: 57.9 us -> 56.3 us  [shards(): pl.pallas_call(functools.partial(kernel, sizes), out_shape=(out, out), in...]
where the time goes in v3:
time: 60.3 us; the launch traced here: 60.1 us
  Pallas kernels  56.3 us (93%)
  local copies, waits for them, and re-layouts  3.11 us (5%)
  between operations  0.65 us (1%)
    pallas_call x1, Pallas kernels, shards(): pl.pallas_call(functools.partial(kernel, sizes), out_shape=(out, out), in...  56.3 us
    unnamed x6, local copies, waits for them, and re-layouts  3.11 us

profile of v3, /device:TPU:0, one launch (start us, length us, event | category | flops | bytes accessed | tf_op | source)
XLA Modules:
  0.0 60.1 jit_solution(4137104703828227481)
XLA Ops:
  0.6 0.0 copy-start
  0.6 0.9 %copy-done = f32[3,8,16,128]{3,2,1,0:T(8,128)S(1)} copy-done((f32[3,8,16,128]{3,2,1,0:T(8,128)S(1)}, f32[3,8,16,128]{3,2,1,0:T(8,128)}, u32[]{:S(2)}) %copy-start) | copy-done | bytes 196632
  1.6 0.0 copy-start.1
  1.6 0.8 %copy-done.1 = f32[8,16,128]{2,1,0:T(8,128)S(1)} copy-done((f32[8,16,128]{2,1,0:T(8,128)S(1)}, f32[8,16,128]{2,1,0:T(8,128)}, u32[]{:S(2)}) %copy-start.1) | copy-done | bytes 65560
  2.4 56.3 %shard_map.41 = (f32[3,8,16,128]{3,2,1,0:T(8,128)S(1)}, f32[3,8,16,128]{3,2,1,0:T(8,128)S(1)}) custom-call(f32[3,8,16,128]{3,2,1,0:T(8,128)S(1)} %copy-done, f32[8,16,128]{2,1,0:T(8,128)S(1)} %copy-done.1), custom_call_target="tpu_custom_call" | custom-call | tf_op jit(solution)/shard_map/pallas_call | solution.py:579
  58.7 0.7 %copy.6 = f32[3,8,16,128]{3,2,1,0:T(8,128)} copy(f32[3,8,16,128]{3,2,1,0:T(8,128)S(1)} %get-tuple-element.4) | data formatting | bytes 393216
  59.4 0.7 %copy.7 = f32[3,8,16,128]{3,2,1,0:T(8,128)} copy(f32[3,8,16,128]{3,2,1,0:T(8,128)S(1)} %get-tuple-element.5) | data formatting | bytes 393216
Async XLA Ops:
  0.6 0.9 %copy-start = (f32[3,8,16,128]{3,2,1,0:T(8,128)S(1)}, f32[3,8,16,128]{3,2,1,0:T(8,128)}, u32[]{:S(2)}) copy-start(f32[3,8,16,128]{3,2,1,0:T(8,128)} %f_ref.1) | copy-start | bytes 589828
  1.6 0.8 %copy-start.1 = (f32[8,16,128]{2,1,0:T(8,128)S(1)}, f32[8,16,128]{2,1,0:T(8,128)}, u32[]{:S(2)}) copy-start(f32[8,16,128]{2,1,0:T(8,128)} %v_ref.1) | copy-start | bytes 196612
